TPU v7x, 32 devices: a whole 2x2x4 slice. The times are simulated.
32 devices in a mesh: group: 4 (over y, core), dev: 8 (over z, x).
Axes of the slice: x: 2, y: 2, z: 4, core: 2. Of those that a mesh axis runs over, the one named last changes fastest.
Arguments:
- points: bfloat16 [8192, 256], P(('group', 'dev')), may hold values from -6 to 6
- base_factor: float32 [8192, 256], P(('group', 'dev')), may hold values from -0.12 to 0.12
- pivots: int32 [2, 64], replicated, may hold values from 0 to 8191, as said below
Outputs:
- new_factor: float32 [8192, 128], P(('group', 'dev'))
- residual_diag: float32 [8192], P(('group', 'dev'))
Inputs may be any that keep to these rules, and one draw needn't show every extreme that they name: `pivots`: all 128 pivot indices are distinct; most of them fall on the points of a few devices.
All inputs are finite; a program needn't handle non-finite values.
Results may differ from a plain program's by a relative error of at most 0.0003.
Values sent between devices are 32-bit elements; how exact they have to be, the bound alone decides.
No kernel may reach another device: no remote copies, remote signals or barrier semaphores. Data moves between devices by JAX's collectives and lax.ppermute only.
A program may use at most 64 MiB of HBM per device.

v0:
```python
import jax
import jax.numpy as jnp
from jax import lax
from jax.sharding import PartitionSpec as P

DIM = 256
PIV = 64
ROUNDS = 2


def kernel_rows(rows, row_norms, centres, centre_norms):
    inner = jnp.dot(rows, centres.T, preferred_element_type=jnp.float32)
    dist = row_norms[:, None] + centre_norms[None, :] - 2.0 * inner
    return jnp.exp(-2.0 * dist / DIM)


def per_device(points, base_factor, pivots):
    local_rows = points.shape[0]
    device = lax.axis_index(("group", "dev"))
    norms = jnp.sum(points.astype(jnp.float32) ** 2, axis=1)
    factor = base_factor
    diag = 1.0 - jnp.sum(base_factor * base_factor, axis=1)
    positions = lax.broadcasted_iota(jnp.int32, (1, local_rows), 1)
    every_offset = pivots.reshape(-1) - device * local_rows
    every_select = (every_offset[:, None] == positions).astype(jnp.float32)
    every_points = jnp.dot(
        every_select.astype(jnp.bfloat16), points, preferred_element_type=jnp.float32
    )
    every_base = jnp.dot(every_select, base_factor, precision=lax.Precision.HIGHEST)
    every_centres, pivot_factor = lax.psum((every_points, every_base), ("group", "dev"))
    every_norms = jnp.sum(every_centres * every_centres, axis=1)
    every_half = every_centres.astype(jnp.bfloat16)
    collected = []
    for step in range(ROUNDS):
        offsets = pivots[step] - device * local_rows
        select = (offsets[:, None] == positions).astype(jnp.float32)
        centres = every_centres[step * PIV : (step + 1) * PIV]
        factor_rows = pivot_factor[step * PIV : (step + 1) * PIV]
        centre_norms = jnp.sum(centres * centres, axis=1)
        centre_half = centres.astype(jnp.bfloat16)
        resid = kernel_rows(points, norms, centre_half, centre_norms) - jnp.dot(
            factor, factor_rows.T, precision=lax.Precision.HIGHEST
        )
        block = lax.psum(jnp.dot(select, resid, precision=lax.Precision.HIGHEST), ("group", "dev"))
        lower = jnp.linalg.cholesky(block)
        inverse = lax.linalg.triangular_solve(
            lower, jnp.eye(block.shape[0], dtype=block.dtype), left_side=True, lower=True
        )
        cols = jnp.dot(resid, inverse.T, precision=lax.Precision.HIGHEST)
        diag = diag - jnp.sum(cols * cols, axis=1)
        factor = jnp.concatenate([factor, cols], axis=1)
        collected.append(cols)
        if step + 1 < ROUNDS:
            pivot_resid = kernel_rows(every_half, every_norms, centre_half, centre_norms) - jnp.dot(
                pivot_factor, factor_rows.T, precision=lax.Precision.HIGHEST
            )
            pivot_cols = jnp.dot(pivot_resid, inverse.T, precision=lax.Precision.HIGHEST)
            pivot_factor = jnp.concatenate([pivot_factor, pivot_cols], axis=1)
    return (jnp.concatenate(collected, axis=1), diag)


def solution(mesh):
    return jax.shard_map(
        per_device,
        mesh=mesh,
        in_specs=(P(("group", "dev"), None), P(("group", "dev"), None), P()),
        out_specs=(P(("group", "dev"), None), P(("group", "dev"))),
        check_vma=False,
    )
```

profile of v0, /device:TPU:0, one launch (start us, length us, event | category | flops | bytes accessed | tf_op | source)
XLA Modules:
  0.0 260.4 jit_solution(3146454910611682736)
XLA Ops:
  7.2 0.7 copy-done.4
  8.0 1.9 fusion.17
  9.9 0.9 fusion.19
  10.9 0.8 copy-done
  11.8 131.9 %all-reduce.3.cloned.1.call-done = (f32[128,256]{1,0:T(8,128)}, f32[128,256]{1,0:T(8,128)}) async-done(((f32[128,256]{1,0:T(8,128)}, f32[128,256]{1,0:T(8,128)}), (f32[128,256]{1,0:T(8,128)}, f32[128,256]{1,0:T(8,128)})) %all-reduce.3.cloned.1.call-update) | async-done | bytes 262160 | tf_op jit(solution)/shard_map/psum | solution.py:30
  143.8 1.0 multiply_reduce_fusion.5
  144.9 0.4 convolution_bitcast_fusion
  145.5 0.2 fusion.23
  145.8 39.4 %psum.30 = f32[64,64]{0,1:T(8,128)S(1)} all-reduce(f32[64,64]{0,1:T(8,128)S(1)} %fusion.23), channel_id=1, replica_groups=mesh['group'=4,'dev'=8] {'group','dev'}, use_global_device_ids=true, to_apply=%region_4.0 | all-reduce | flops 4096 | bytes 32768 | tf_op jit(solution)/shard_map/psum | solution.py:44
  185.3 5.8 %cholesky.44 = f32[64,64]{1,0:T(8,128)S(1)} custom-call(f32[64,64]{1,0:T(8,128)S(1)} %fusion.36), custom_call_target="Cholesky" | custom-call | tf_op jit(solution)/shard_map/jit(cholesky)/cholesky | solution.py:45
  191.2 0.6 compare_reduce_fusion.1
  191.8 0.7 fusion.31
  192.5 4.9 %custom-call.6 = f32[1,64,64]{1,2,0:T(8,128)S(1)} custom-call(f32[1,64,64]{2,1,0:T(8,128)S(1)} %fusion.31), custom_call_target="InvertDiagBlocksLowerTriangular" | custom-call | tf_op jit(solution)/shard_map/triangular_solve/custom-call.0 | solution.py:46
  197.4 0.3 fusion.29
  197.8 0.3 convolution_subtract_fusion
  198.6 0.5 fusion.13
  199.5 40.0 %psum.31 = f32[64,64]{0,1:T(8,128)S(1)} all-reduce(f32[64,64]{0,1:T(8,128)S(1)} %fusion.24), channel_id=1, replica_groups=mesh['group'=4,'dev'=8] {'group','dev'}, use_global_device_ids=true, to_apply=%region_9.12 | all-reduce | flops 4096 | bytes 32768 | tf_op jit(solution)/shard_map/psum | solution.py:44
  239.7 5.8 %cholesky.55 = f32[64,64]{1,0:T(8,128)S(1)} custom-call(f32[64,64]{1,0:T(8,128)S(1)} %fusion.34), custom_call_target="Cholesky" | custom-call | tf_op jit(solution)/shard_map/jit(cholesky)/cholesky | solution.py:45
  245.6 0.6 compare_reduce_fusion
  246.2 0.7 fusion.32
  246.9 4.9 %custom-call.7 = f32[1,64,64]{1,2,0:T(8,128)S(1)} custom-call(f32[1,64,64]{2,1,0:T(8,128)S(1)} %fusion.32), custom_call_target="InvertDiagBlocksLowerTriangular" | custom-call | tf_op jit(solution)/shard_map/triangular_solve/custom-call.0 | solution.py:46
  251.8 0.3 fusion.27
  252.3 0.8 copy.10
  253.0 0.6 subtract_subtract_fusion
  (31 shorter events, 2.3 us)
Async XLA Ops:
  7.2 136.6 %all-reduce.3.cloned.1.call-start = ((), (), s32[]{:S(2)}) async-start(), calls=%async_computation | async-start | bytes 524288 | tf_op jit(solution)/shard_map/psum | solution.py:30
  7.2 0.7 copy-start.4
  8.0 1.9 copy-start.2
  10.8 0.9 copy-start
  143.8 1.0 copy-start.1
  143.8 1.1 copy-start.3
Sparse Core Ops, SparseCore 0:
  14.2 129.4 all-reduce.2
where the time goes:
time: 261 us; the launch traced here: 260 us
  waiting for transfers between devices  132 us (51%)
  blocking collectives  79.5 us (30%)
  other arithmetic  26.1 us (10%)
  between operations  14.2 us (5%)
  matrix products  6.1 us (2%)
    psum x1, waiting for transfers between devices, per_device(): lax.psum((every_points, every_base), ('group', 'dev'))  132 us
    psum x2, blocking collectives, per_device(): lax.psum(jnp.dot(select, resid, precision=lax.Precision.HIGHEST), ('group...  79.5 us
    another operation x6, other arithmetic, per_device(): lower = jnp.linalg.cholesky(block)  13 us
    another operation x4, other arithmetic, per_device(): lax.linalg.triangular_solve(lower, jnp.eye(block.shape[0], dtype=block.dt...  11.1 us
  transfers between devices with their start and end apart: 1, of which 1 were waited for; matrix products, arithmetic and copies ran while one was open for 0% of the time, Pallas kernels for 0%

commit v1 on v0

--- a/solution.py
+++ b/solution.py
@@ -27,7 +27,7 @@
         every_select.astype(jnp.bfloat16), points, preferred_element_type=jnp.float32
     )
     every_base = jnp.dot(every_select, base_factor, precision=lax.Precision.HIGHEST)
-    every_centres, pivot_factor = lax.psum((every_points, every_base), ("group", "dev"))
+    every_centres, pivot_factor = lax.psum(lax.psum((every_points, every_base), "dev"), "group")
     every_norms = jnp.sum(every_centres * every_centres, axis=1)
     every_half = every_centres.astype(jnp.bfloat16)
     collected = []

time: 261 us -> 238 us (0.912)
  waiting for transfers between devices: 132 us -> 109 us
    psum x1 -> x2, waiting for transfers between devices: 132 us -> 109 us  [the longest x1 75.3 us: per_device(): lax.psum((every_points, every_base), 'dev')]
  transfers between devices with their start and end apart: 1 -> 2, of which waited for: 1 -> 2; matrix products, arithmetic and copies ran while one was open for 0% -> 0% of each run, Pallas kernels for 0% -> 0%
where the time goes in v1:
time: 238 us
  waiting for transfers between devices  109 us (46%)
  blocking collectives  80.6 us (34%)
  other arithmetic  26.1 us (11%)
  between operations  14.3 us (6%)
  matrix products  6.11 us (3%)
    psum x2, blocking collectives, per_device(): lax.psum(jnp.dot(select, resid, precision=lax.Precision.HIGHEST), ('group...  80.6 us
    psum x1, waiting for transfers between devices, per_device(): lax.psum((every_points, every_base), 'dev')  75.3 us
    psum x1, waiting for transfers between devices, per_device(): lax.psum(lax.psum((every_points, every_base), 'dev'), 'group')  33.8 us
    another operation x6, other arithmetic, per_device(): lower = jnp.linalg.cholesky(block)  13 us
    another operation x4, other arithmetic, per_device(): lax.linalg.triangular_solve(lower, jnp.eye(block.shape[0], dtype=block.dt...  11.1 us
  transfers between devices with their start and end apart: 2, of which 2 were waited for; matrix products, arithmetic and copies ran while one was open for 0% of the time, Pallas kernels for 0%

profile of v1, /device:TPU:0, one launch (start us, length us, event | category | flops | bytes accessed | tf_op | source)
XLA Modules:
  0.0 237.9 jit_solution(8450884477207807933)
XLA Ops:
  7.2 0.7 copy-done.4
  8.0 1.9 fusion.17
  9.9 0.9 fusion.19
  10.9 75.3 %all-reduce.5.cloned.1.call-done = (f32[128,256]{1,0:T(8,128)}, f32[128,256]{1,0:T(8,128)}) async-done(((f32[128,256]{1,0:T(8,128)}, f32[128,256]{1,0:T(8,128)}), (f32[128,256]{1,0:T(8,128)}, f32[128,256]{1,0:T(8,128)})) %all-reduce.5.cloned.1.call-update) | async-done | bytes 262160 | tf_op jit(solution)/shard_map/psum | solution.py:30
  86.4 33.8 %all-reduce.7.cloned.1.call-done = (f32[128,256]{1,0:T(8,128)}, f32[128,256]{1,0:T(8,128)}) async-done(((f32[128,256]{1,0:T(8,128)}, f32[128,256]{1,0:T(8,128)}), (f32[128,256]{1,0:T(8,128)}, f32[128,256]{1,0:T(8,128)})) %all-reduce.7.cloned.1.call-update) | async-done | bytes 262160 | tf_op jit(solution)/shard_map/psum | solution.py:30
  120.2 1.0 multiply_reduce_fusion.5
  121.3 0.4 convolution_bitcast_fusion
  121.9 0.3 convolution_subtract_fusion
  122.3 0.2 fusion.23
  122.6 39.4 %psum.46 = f32[64,64]{0,1:T(8,128)S(1)} all-reduce(f32[64,64]{0,1:T(8,128)S(1)} %fusion.23), channel_id=1, replica_groups=mesh['group'=4,'dev'=8] {'group','dev'}, use_global_device_ids=true, to_apply=%region_6.0 | all-reduce | flops 4096 | bytes 32768 | tf_op jit(solution)/shard_map/psum | solution.py:44
  162.1 5.8 %cholesky.44 = f32[64,64]{1,0:T(8,128)S(1)} custom-call(f32[64,64]{1,0:T(8,128)S(1)} %fusion.36), custom_call_target="Cholesky" | custom-call | tf_op jit(solution)/shard_map/jit(cholesky)/cholesky | solution.py:45
  168.0 0.6 compare_reduce_fusion.1
  168.7 0.7 fusion.31
  169.3 4.9 %custom-call.6 = f32[1,64,64]{1,2,0:T(8,128)S(1)} custom-call(f32[1,64,64]{2,1,0:T(8,128)S(1)} %fusion.31), custom_call_target="InvertDiagBlocksLowerTriangular" | custom-call | tf_op jit(solution)/shard_map/triangular_solve/custom-call.0 | solution.py:46
  174.2 0.3 fusion.29
  175.0 0.5 fusion.13
  176.0 41.1 %psum.47 = f32[64,64]{0,1:T(8,128)S(1)} all-reduce(f32[64,64]{0,1:T(8,128)S(1)} %fusion.24), channel_id=1, replica_groups=mesh['group'=4,'dev'=8] {'group','dev'}, use_global_device_ids=true, to_apply=%region_11.14 | all-reduce | flops 4096 | bytes 32768 | tf_op jit(solution)/shard_map/psum | solution.py:44
  217.2 5.8 %cholesky.55 = f32[64,64]{1,0:T(8,128)S(1)} custom-call(f32[64,64]{1,0:T(8,128)S(1)} %fusion.34), custom_call_target="Cholesky" | custom-call | tf_op jit(solution)/shard_map/jit(cholesky)/cholesky | solution.py:45
  223.1 0.6 compare_reduce_fusion
  223.7 0.7 fusion.32
  224.4 4.9 %custom-call.7 = f32[1,64,64]{1,2,0:T(8,128)S(1)} custom-call(f32[1,64,64]{2,1,0:T(8,128)S(1)} %fusion.32), custom_call_target="InvertDiagBlocksLowerTriangular" | custom-call | tf_op jit(solution)/shard_map/triangular_solve/custom-call.0 | solution.py:46
  229.3 0.3 fusion.27
  229.8 0.8 copy.10
  230.5 0.6 subtract_subtract_fusion
  (34 shorter events, 2.3 us)
Async XLA Ops:
  7.2 79.0 %all-reduce.5.cloned.1.call-start = ((), (), s32[]{:S(2)}) async-start(), calls=%async_computation | async-start | bytes 524288 | tf_op jit(solution)/shard_map/psum | solution.py:30
  7.2 0.7 copy-start.4
  8.0 1.9 copy-start.2
  10.8 75.5 %copy-start = (f32[256,256]{1,0:T(8,128)S(1)}, f32[256,256]{1,0:T(8,128)}, u32[]{:S(2)}) copy-start(f32[256,256]{1,0:T(8,128)} %param.7) | copy-start | bytes 786436
  10.8 109.4 %all-reduce.7.cloned.1.call-start = ((), (), s32[]{:S(2)}) async-start(), calls=%async_computation.1 | async-start | bytes 524288 | tf_op jit(solution)/shard_map/psum | solution.py:30
  120.2 1.0 copy-start.1
  120.2 1.1 copy-start.3
Sparse Core Ops, SparseCore 0:
  12.0 74.0 all-reduce.4
  88.5 31.5 all-reduce.6

commit v2 on v0

--- a/solution.py
+++ b/solution.py
@@ -41,7 +41,12 @@
         resid = kernel_rows(points, norms, centre_half, centre_norms) - jnp.dot(
             factor, factor_rows.T, precision=lax.Precision.HIGHEST
         )
-        block = lax.psum(jnp.dot(select, resid, precision=lax.Precision.HIGHEST), ("group", "dev"))
+        block = jnp.sum(
+            lax.all_gather(
+                jnp.dot(select, resid, precision=lax.Precision.HIGHEST), ("group", "dev")
+            ),
+            axis=0,
+        )
         lower = jnp.linalg.cholesky(block)
         inverse = lax.linalg.triangular_solve(
             lower, jnp.eye(block.shape[0], dtype=block.dtype), left_side=True, lower=True

time: 261 us -> 323 us (1.24)
  blocking collectives: 79.5 us -> 142 us
    all_gather x0 -> x2, blocking collectives: none -> 142 us  [per_device(): lax.all_gather(jnp.dot(select, resid, precision=lax.Precision.HIGHEST), (...]
    psum x2 -> x0, blocking collectives: 79.5 us -> none  [per_device(): lax.psum(jnp.dot(select, resid, precision=lax.Precision.HIGHEST), ('group...]
where the time goes in v2:
time: 323 us
  blocking collectives  142 us (44%)
  waiting for transfers between devices  132 us (41%)
  other arithmetic  26.3 us (8%)
  between operations  14.2 us (4%)
  matrix products  6.07 us (2%)
    all_gather x2, blocking collectives, per_device(): lax.all_gather(jnp.dot(select, resid, precision=lax.Precision.HIGHEST), (...  142 us
    psum x1, waiting for transfers between devices, per_device(): lax.psum((every_points, every_base), ('group', 'dev'))  132 us
    another operation x6, other arithmetic, per_device(): lower = jnp.linalg.cholesky(block)  13 us
    another operation x4, other arithmetic, per_device(): lax.linalg.triangular_solve(lower, jnp.eye(block.shape[0], dtype=block.dt...  11.1 us
  transfers between devices with their start and end apart: 1, of which 1 were waited for; matrix products, arithmetic and copies ran while one was open for 0% of the time, Pallas kernels for 0%

profile of v2, /device:TPU:0, one launch (start us, length us, event | category | flops | bytes accessed | tf_op | source)
XLA Modules:
  0.0 322.7 jit_solution(9368908212899809395)
XLA Ops:
  7.2 0.7 copy-done.4
  8.0 1.9 fusion.17
  9.9 0.9 fusion.19
  10.9 0.8 copy-done
  11.8 131.9 %all-reduce.3.cloned.1.call-done = (f32[128,256]{1,0:T(8,128)}, f32[128,256]{1,0:T(8,128)}) async-done(((f32[128,256]{1,0:T(8,128)}, f32[128,256]{1,0:T(8,128)}), (f32[128,256]{1,0:T(8,128)}, f32[128,256]{1,0:T(8,128)})) %all-reduce.3.cloned.1.call-update) | async-done | bytes 262160 | tf_op jit(solution)/shard_map/psum | solution.py:30
  143.8 1.0 multiply_reduce_fusion.5
  144.9 0.4 convolution_bitcast_fusion
  145.5 0.2 fusion.23
  145.7 71.4 %all-gather = f32[2048,64]{1,0:T(8,128)S(1)} all-gather(f32[64,64]{1,0:T(8,128)S(1)} %fusion.23), channel_id=2, replica_groups=mesh['group'=4,'dev'=8] {'group','dev'}, dimensions={0}, use_global_device_ids=true | all-gather | bytes 540672 | tf_op jit(solution)/shard_map/all_gather | solution.py:45
  217.3 5.8 %cholesky.44 = f32[64,64]{1,0:T(8,128)S(1)} custom-call(f32[64,64]{1,0:T(8,128)S(1)} %fusion.36), custom_call_target="Cholesky" | custom-call | tf_op jit(solution)/shard_map/jit(cholesky)/cholesky | solution.py:50
  223.2 0.6 compare_reduce_fusion.1
  223.8 0.7 fusion.31
  224.5 4.9 %custom-call.6 = f32[1,64,64]{1,2,0:T(8,128)S(1)} custom-call(f32[1,64,64]{2,1,0:T(8,128)S(1)} %fusion.31), custom_call_target="InvertDiagBlocksLowerTriangular" | custom-call | tf_op jit(solution)/shard_map/triangular_solve/custom-call.0 | solution.py:51
  229.4 0.3 fusion.29
  229.8 0.3 convolution_subtract_fusion
  230.6 0.5 fusion.13
  231.6 70.2 %all-gather.1 = f32[2048,64]{1,0:T(8,128)S(1)} all-gather(f32[64,64]{1,0:T(8,128)S(1)} %fusion.24), channel_id=3, replica_groups=mesh['group'=4,'dev'=8] {'group','dev'}, dimensions={0}, use_global_device_ids=true | all-gather | bytes 540672 | tf_op jit(solution)/shard_map/all_gather | solution.py:45
  301.9 5.8 %cholesky.55 = f32[64,64]{1,0:T(8,128)S(1)} custom-call(f32[64,64]{1,0:T(8,128)S(1)} %fusion.34), custom_call_target="Cholesky" | custom-call | tf_op jit(solution)/shard_map/jit(cholesky)/cholesky | solution.py:50
  307.8 0.6 compare_reduce_fusion
  308.5 0.7 fusion.32
  309.1 4.9 %custom-call.7 = f32[1,64,64]{1,2,0:T(8,128)S(1)} custom-call(f32[1,64,64]{2,1,0:T(8,128)S(1)} %fusion.32), custom_call_target="InvertDiagBlocksLowerTriangular" | custom-call | tf_op jit(solution)/shard_map/triangular_solve/custom-call.0 | solution.py:51
  314.0 0.3 fusion.27
  314.5 0.8 copy.12
  315.3 0.6 subtract_subtract_fusion
  (33 shorter events, 2.4 us)
Async XLA Ops:
  7.2 136.6 %all-reduce.3.cloned.1.call-start = ((), (), s32[]{:S(2)}) async-start(), calls=%async_computation | async-start | bytes 524288 | tf_op jit(solution)/shard_map/psum | solution.py:30
  7.2 0.7 copy-start.4
  8.0 1.9 copy-start.2
  10.8 0.9 copy-start
  143.8 1.0 copy-start.1
  143.8 1.1 copy-start.3
Sparse Core Ops, SparseCore 0:
  14.2 129.4 all-reduce.2
